TPU v7x, 32 devices: a whole 2x2x4 slice. The times are simulated.
32 devices in a mesh: dp: 4 (over z), ctx: 2 (over x), tp: 4 (over y, core).
Axes of the slice: x: 2, y: 2, z: 4, core: 2. Of those that a mesh axis runs over, the one named last changes fastest.
Arguments:
- tokens: bfloat16 [4096, 2048], P(('dp', 'ctx')), may hold values from -6 to 6
- segments: int32 [4, 1024], P('dp'), may hold values from 0 to 3, never falling along the last dimension, each value on 1 to 512 neighbouring positions
- attn_gain: float32 [2048], replicated, may hold values from 0.5 to 1.5
- query_weight: bfloat16 [2048, 2048], P(None, 'tp'), may hold values from -0.125 to 0.125
- key_weight: bfloat16 [2048, 256], P(None, 'tp'), may hold values from -0.125 to 0.125
- value_weight: bfloat16 [2048, 256], P(None, 'tp'), may hold values from -0.125 to 0.125
- output_weight: bfloat16 [2048, 2048], P('tp'), may hold values from -2 to 2
- mlp_gain: float32 [2048], replicated, may hold values from 0.5 to 1.5
- gate_weight: bfloat16 [2048, 5632], P(None, 'tp'), may hold values from -0.125 to 0.125
- up_weight: bfloat16 [2048, 5632], P(None, 'tp'), may hold values from -0.125 to 0.125
- down_weight: bfloat16 [5632, 2048], P('tp'), may hold values from -0.078125 to 0.078125
- cotangent: bfloat16 [4096, 2048], P(('dp', 'ctx')), may hold values from -6 to 6
Outputs:
- layer_out: float32 [4096, 2048], P(('dp', 'ctx'))
- tokens_grad: float32 [4096, 2048], P(('dp', 'ctx'))
- attn_gain_grad: float32 [2048], P(('dp', 'ctx'))
- query_grad: float32 [2048, 2048], P(('dp', 'ctx'), 'tp')
- key_grad: float32 [2048, 256], P(('dp', 'ctx'), 'tp')
- value_grad: float32 [2048, 256], P(('dp', 'ctx'), 'tp')
- output_grad: float32 [2048, 2048], P('tp', ('dp', 'ctx'))
- mlp_gain_grad: float32 [2048], P(('dp', 'ctx'))
- gate_grad: float32 [2048, 5632], P(('dp', 'ctx'), 'tp')
- up_grad: float32 [2048, 5632], P(('dp', 'ctx'), 'tp')
- down_grad: float32 [5632, 2048], P('tp', ('dp', 'ctx'))
Inputs may be any that keep to these rules, and one draw needn't show every extreme that they name: `segments`: along each packed sequence the document numbers never fall; a document has 1 to 512 tokens, and one document of each sequence has exactly 512.
All inputs are finite; a program needn't handle non-finite values.
Results may differ from a plain program's by a relative error of at most 0.013.
Values may be sent and summed in bfloat16 or wider, within the bound.
A program may use at most 192 MiB of HBM per device.

v0:
```python
import jax
import jax.numpy as jnp
from jax import lax
from jax.sharding import PartitionSpec as P

HEAD = 64
EPSILON = 1e-05
MASKED = -1000000000.0


def contract(left_side, right_side, left_dim, right_dim):
    return lax.dot_general(
        left_side,
        right_side,
        (((left_dim,), (right_dim,)), ((), ())),
        preferred_element_type=jnp.float32,
    )


def rms_parts(values, gain_vec):
    inverse = lax.rsqrt(jnp.mean(values * values, axis=-1, keepdims=True) + EPSILON)
    normed = values * inverse
    return (normed, inverse, (normed * gain_vec).astype(jnp.bfloat16))


def rms_back(grad_out, normed, inverse, gain_vec):
    scaled = grad_out * gain_vec
    input_back = inverse * (scaled - normed * jnp.mean(scaled * normed, axis=-1, keepdims=True))
    return (input_back, jnp.sum(grad_out * normed, axis=0))


def rope_tables(positions, head_width):
    frequency = 10000.0 ** (-jnp.arange(0, head_width, 2, dtype=jnp.float32) / head_width)
    angles = positions.astype(jnp.float32)[:, None] * frequency[None, :]
    cos_table = jnp.concatenate([jnp.cos(angles), jnp.cos(angles)], -1)
    sin_table = jnp.concatenate([jnp.sin(angles), jnp.sin(angles)], -1)
    return (cos_table, sin_table)


def rotate(values, cos_table, sin_table):
    half_width = values.shape[-1] // 2
    turned = jnp.concatenate([-values[..., half_width:], values[..., :half_width]], -1)
    return values * cos_table[:, None, :] + turned * sin_table[:, None, :]


def rotate_back(gradients, cos_table, sin_table):
    half_width = gradients.shape[-1] // 2
    scaled = gradients * sin_table[:, None, :]
    turned = jnp.concatenate([scaled[..., half_width:], -scaled[..., :half_width]], -1)
    return gradients * cos_table[:, None, :] + turned


def block_scores(queries, keys_blk, allowed, score_scale):
    raw_scores = (
        jnp.einsum("bgnd,kgd->gnbk", queries, keys_blk, preferred_element_type=jnp.float32)
        * score_scale
    )
    return jnp.where(allowed[None, None], raw_scores, MASKED)


def shards(
    tokens,
    segments,
    attn_gain,
    query_weight,
    key_weight,
    value_weight,
    output_weight,
    mlp_gain,
    gate_weight,
    up_weight,
    down_weight,
    cotangent,
):
    row_count = tokens.shape[0]
    kv_local = key_weight.shape[1] // HEAD
    q_local = query_weight.shape[1] // HEAD
    groups = q_local // kv_local
    kv_width = kv_local * HEAD
    score_scale = HEAD ** (-0.5)
    ctx_rank = lax.axis_index("ctx")
    ctx_count = lax.axis_size("ctx")
    offsets = jnp.arange(row_count, dtype=jnp.int32)
    query_pos = ctx_rank * row_count + offsets
    seq_segs = segments[0]
    seq_rows = seq_segs.shape[0]
    query_segs = lax.dynamic_slice_in_dim(seq_segs, ctx_rank * row_count, row_count)
    cos_table, sin_table = rope_tables(query_pos, HEAD)
    tokens_wide = tokens.astype(jnp.float32)
    normed_one, inverse_one, attn_in = rms_parts(tokens_wide, attn_gain)
    queries = contract(attn_in, query_weight, 1, 0).reshape(row_count, q_local, HEAD)
    keys_pre = contract(attn_in, key_weight, 1, 0).reshape(row_count, kv_local, HEAD)
    values_pre = contract(attn_in, value_weight, 1, 0)
    queries_rot = (
        rotate(queries, cos_table, sin_table)
        .astype(jnp.bfloat16)
        .reshape(row_count, kv_local, groups, HEAD)
    )
    keys_rot = (
        rotate(keys_pre, cos_table, sin_table).astype(jnp.bfloat16).reshape(row_count, kv_width)
    )
    local_kv = jnp.concatenate([keys_rot, values_pre.astype(jnp.bfloat16)], axis=1)
    whole_kv = lax.all_gather(local_kv, "ctx", axis=0, tiled=True)

    def key_block(kv_rows_all, block_index):
        first_row = block_index * row_count
        kv_piece = lax.dynamic_slice_in_dim(kv_rows_all, first_row, row_count, 0)
        key_segs = lax.dynamic_slice_in_dim(seq_segs, first_row, row_count)
        allowed = (query_segs[:, None] == key_segs[None, :]) & (
            (first_row + offsets)[None, :] <= query_pos[:, None]
        )
        keys_blk = kv_piece[:, :kv_width].reshape(row_count, kv_local, HEAD)
        values_blk = kv_piece[:, kv_width:].reshape(row_count, kv_local, HEAD)
        return (keys_blk, values_blk, allowed)

    def max_step(block_index, state_pair):
        running_max, running_sum = state_pair
        keys_blk, values_blk, allowed = key_block(whole_kv, block_index)
        scores = block_scores(queries_rot, keys_blk, allowed, score_scale)
        new_max = jnp.maximum(running_max, jnp.max(scores, axis=-1))
        new_sum = running_sum * jnp.exp(running_max - new_max) + jnp.sum(
            jnp.exp(scores - new_max[..., None]), axis=-1
        )
        return (new_max, new_sum)

    start_max = jnp.full((kv_local, groups, row_count), MASKED, jnp.float32)
    row_max, row_sum = lax.fori_loop(0, ctx_count, max_step, (start_max, jnp.zeros_like(start_max)))
    log_total = row_max + jnp.log(row_sum)

    def out_step(block_index, mixed_heads):
        keys_blk, values_blk, allowed = key_block(whole_kv, block_index)
        soft_weights = jnp.exp(
            block_scores(queries_rot, keys_blk, allowed, score_scale) - log_total[..., None]
        ).astype(jnp.bfloat16)
        return mixed_heads + jnp.einsum(
            "gnbk,kgd->bgnd", soft_weights, values_blk, preferred_element_type=jnp.float32
        )

    mixed_heads = lax.fori_loop(
        0, ctx_count, out_step, jnp.zeros((row_count, kv_local, groups, HEAD), jnp.float32)
    )
    heads_out = mixed_heads.reshape(row_count, q_local * HEAD).astype(jnp.bfloat16)
    branch = lax.psum(contract(heads_out, output_weight, 1, 0), "tp")
    middle = tokens_wide + branch
    normed_two, inverse_two, mlp_in = rms_parts(middle, mlp_gain)
    gate_pre = contract(mlp_in, gate_weight, 1, 0)
    up_pre = contract(mlp_in, up_weight, 1, 0)
    sigmoid_gate = jax.nn.sigmoid(gate_pre)
    silu_gate = gate_pre * sigmoid_gate
    hidden = (silu_gate * up_pre).astype(jnp.bfloat16)
    layer_out = middle + lax.psum(
        contract(hidden, down_weight, 1, 0).astype(jnp.bfloat16), "tp"
    ).astype(jnp.float32)
    cot_wide = cotangent.astype(jnp.float32)
    down_grad = contract(hidden, cotangent, 0, 0)
    hidden_back = contract(cotangent, down_weight, 1, 1)
    gate_back = (
        hidden_back * up_pre * sigmoid_gate * (1.0 + gate_pre * (1.0 - sigmoid_gate))
    ).astype(jnp.bfloat16)
    up_back = (hidden_back * silu_gate).astype(jnp.bfloat16)
    gate_grad = contract(mlp_in, gate_back, 0, 0)
    up_grad = contract(mlp_in, up_back, 0, 0)
    mlp_in_back = lax.psum(
        contract(gate_back, gate_weight, 1, 1) + contract(up_back, up_weight, 1, 1), "tp"
    )
    middle_part, mlp_gain_grad = rms_back(mlp_in_back, normed_two, inverse_two, mlp_gain)
    middle_back = cot_wide + middle_part
    mlp_done = (gate_grad, up_grad, down_grad, mlp_gain_grad)
    branch_back = middle_back.astype(jnp.bfloat16)
    output_grad = contract(heads_out, branch_back, 0, 0)
    heads_back = (
        contract(branch_back, output_weight, 1, 1)
        .astype(jnp.bfloat16)
        .reshape(row_count, kv_local, groups, HEAD)
    )

    def delta_step(block_index, delta_rows):
        keys_blk, values_blk, allowed = key_block(whole_kv, block_index)
        soft_weights = jnp.exp(
            block_scores(queries_rot, keys_blk, allowed, score_scale) - log_total[..., None]
        )
        weight_back = jnp.einsum(
            "bgnd,kgd->gnbk", heads_back, values_blk, preferred_element_type=jnp.float32
        )
        return delta_rows + jnp.sum(soft_weights * weight_back, axis=-1)

    delta_rows = lax.fori_loop(
        0, ctx_count, delta_step, jnp.zeros((kv_local, groups, row_count), jnp.float32)
    )

    def grad_step(block_index, state_pair):
        query_acc, kv_acc = state_pair
        keys_blk, values_blk, allowed = key_block(whole_kv, block_index)
        soft_weights = jnp.exp(
            block_scores(queries_rot, keys_blk, allowed, score_scale) - log_total[..., None]
        )
        weight_back = jnp.einsum(
            "bgnd,kgd->gnbk", heads_back, values_blk, preferred_element_type=jnp.float32
        )
        score_back = (soft_weights * (weight_back - delta_rows[..., None])).astype(jnp.bfloat16)
        query_acc = (
            query_acc
            + jnp.einsum("gnbk,kgd->bgnd", score_back, keys_blk, preferred_element_type=jnp.float32)
            * score_scale
        )
        key_part = (
            jnp.einsum(
                "gnbk,bgnd->kgd", score_back, queries_rot, preferred_element_type=jnp.float32
            )
            * score_scale
        )
        value_part = jnp.einsum(
            "gnbk,bgnd->kgd",
            soft_weights.astype(jnp.bfloat16),
            heads_back,
            preferred_element_type=jnp.float32,
        )
        both_parts = jnp.concatenate(
            [key_part.reshape(row_count, kv_width), value_part.reshape(row_count, kv_width)], axis=1
        )
        first_row = block_index * row_count
        updated = lax.dynamic_slice_in_dim(kv_acc, first_row, row_count, 0) + both_parts
        kv_acc = lax.dynamic_update_slice_in_dim(kv_acc, updated, first_row, 0)
        return (query_acc, kv_acc)

    start_query = jnp.zeros((row_count, kv_local, groups, HEAD), jnp.float32)
    start_kv = jnp.zeros((seq_rows, 2 * kv_width), jnp.float32)
    query_acc, kv_acc = lax.fori_loop(0, ctx_count, grad_step, (start_query, start_kv))
    kv_grad = lax.psum_scatter(kv_acc, "ctx", scatter_dimension=0, tiled=True)
    key_back = (
        rotate_back(kv_grad[:, :kv_width].reshape(row_count, kv_local, HEAD), cos_table, sin_table)
        .reshape(row_count, kv_width)
        .astype(jnp.bfloat16)
    )
    value_back = kv_grad[:, kv_width:].astype(jnp.bfloat16)
    query_back = (
        rotate_back(query_acc.reshape(row_count, q_local, HEAD), cos_table, sin_table)
        .reshape(row_count, q_local * HEAD)
        .astype(jnp.bfloat16)
    )
    query_grad = contract(attn_in, query_back, 0, 0)
    key_grad = contract(attn_in, key_back, 0, 0)
    value_grad = contract(attn_in, value_back, 0, 0)
    attn_in_back = lax.psum(
        contract(query_back, query_weight, 1, 1)
        + contract(key_back, key_weight, 1, 1)
        + contract(value_back, value_weight, 1, 1),
        "tp",
    )
    tokens_part, attn_gain_grad = rms_back(attn_in_back, normed_one, inverse_one, attn_gain)
    tokens_grad = middle_back + tokens_part
    finals = (
        lax.psum_scatter(attn_gain_grad, ("dp", "ctx"), scatter_dimension=0, tiled=True),
        lax.psum_scatter(query_grad, ("dp", "ctx"), scatter_dimension=0, tiled=True),
        lax.psum_scatter(key_grad, ("dp", "ctx"), scatter_dimension=0, tiled=True),
        lax.psum_scatter(value_grad, ("dp", "ctx"), scatter_dimension=0, tiled=True),
        lax.psum_scatter(output_grad, ("dp", "ctx"), scatter_dimension=1, tiled=True),
        lax.psum_scatter(mlp_done[3], ("dp", "ctx"), scatter_dimension=0, tiled=True),
        lax.psum_scatter(mlp_done[0], ("dp", "ctx"), scatter_dimension=0, tiled=True),
        lax.psum_scatter(mlp_done[1], ("dp", "ctx"), scatter_dimension=0, tiled=True),
        lax.psum_scatter(mlp_done[2], ("dp", "ctx"), scatter_dimension=1, tiled=True),
    )
    return (
        layer_out,
        tokens_grad,
        finals[0],
        finals[1],
        finals[2],
        finals[3],
        finals[4],
        finals[5],
        finals[6],
        finals[7],
        finals[8],
    )


def solution(mesh):
    return jax.shard_map(
        shards,
        mesh=mesh,
        in_specs=(
            P(("dp", "ctx"), None),
            P("dp", None),
            P(),
            P(None, "tp"),
            P(None, "tp"),
            P(None, "tp"),
            P("tp", None),
            P(),
            P(None, "tp"),
            P(None, "tp"),
            P("tp", None),
            P(("dp", "ctx"), None),
        ),
        out_specs=(
            P(("dp", "ctx"), None),
            P(("dp", "ctx"), None),
            P(("dp", "ctx")),
            P(("dp", "ctx"), "tp"),
            P(("dp", "ctx"), "tp"),
            P(("dp", "ctx"), "tp"),
            P("tp", ("dp", "ctx")),
            P(("dp", "ctx")),
            P(("dp", "ctx"), "tp"),
            P(("dp", "ctx"), "tp"),
            P("tp", ("dp", "ctx")),
        ),
        check_vma=False,
    )
```

profile of v0, /device:TPU:0, one launch (start us, length us, event | category | flops | bytes accessed | tf_op | source)
XLA Modules:
  0.0 1377.9 jit_solution(10986597939069724232)
XLA Ops:
  14.9 7.3 all_gather.3
  27.9 11.2 while.60
  39.8 12.4 while.61
  47.0 5.1 fusion.177
  57.0 86.9 %all-reduce.8.cloned.1.call-done = f32[512,2048]{1,0:T(8,128)} async-done(((f32[512,2048]{1,0:T(8,128)}), f32[512,2048]{1,0:T(8,128)}) %all-reduce.8.cloned.1.call-update) | async-done | bytes 4194320 | tf_op jit(solution)/shard_map/psum | solution.py:143
  147.9 10.0 fusion.104
  158.0 5.0 fusion.103
  163.0 8.0 multiply_convert_fusion.1
  171.0 4.9 fusion.105
  176.0 5.0 convolution_add_fusion
  181.1 7.8 convolution_convert_fusion
  189.4 77.4 %all-reduce.12.cloned.1.call-done = f32[512,2048]{1,0:T(8,128)} async-done(((f32[512,2048]{1,0:T(8,128)}), f32[512,2048]{1,0:T(8,128)}) %all-reduce.12.cloned.1.call-update) | async-done | bytes 4194320 | tf_op jit(solution)/shard_map/psum | solution.py:163
  266.8 5.0 multiply_reduce_fusion
  271.9 48.9 %all-reduce.10.cloned.1.call-done = bf16[512,2048]{1,0:T(8,128)(2,1)} async-done(((bf16[512,2048]{1,0:T(8,128)(2,1)}), bf16[512,2048]{1,0:T(8,128)(2,1)}) %all-reduce.10.cloned.1.call-update) | async-done | bytes 2097168 | tf_op jit(solution)/shard_map/psum | solution.py:151
  320.7 7.0 multiply_add_fusion
  329.7 9.2 while.62
  339.6 18.1 %while.63 = (s32[]{:T(128)}, f32[512,1,8,64]{0,3,2,1:T(8,128)S(1)}, f32[1024,128]{0,1:T(8,128)S(1)}, bf16[1024,128]{0,1:T(8,128)(2,1)S(1)}, s32[512]{0:T(512)S(1...) while((s32[]{:T(128)}, f32[512,1,8,64]{0,3,2,1:T(8,128)S(1)}, ...), condition=%wide.region_16.17_spmd.clone, body=%wide.region_15.16_spmd.clone.sunk | while | flops 1364886528 | bytes 44171576 | solution.py:228
  363.6 9.8 reduce-scatter.9.cloned.1.call-done
  387.7 5.5 fusion.89
  395.4 6.2 fusion.110
  403.0 6.2 fusion.109
  411.2 6.1 fusion.111
  419.2 45.6 %all-reduce.14.cloned.1.call-done = f32[512,2048]{1,0:T(8,128)} async-done(((f32[512,2048]{1,0:T(8,128)}), f32[512,2048]{1,0:T(8,128)}) %all-reduce.14.cloned.1.call-update) | async-done | bytes 4194320 | tf_op jit(solution)/shard_map/psum | solution.py:244
  468.1 37.2 %all-reduce.2 = (f32[2048]{0:T(1024)S(1)}, f32[2048]{0:T(1024)S(1)}) all-reduce(f32[2048]{0:T(1024)S(1)} %get-tuple-element.837, f32[2048]{0:T(1024)S(1)} %copy-done.39), channel_id=3, replica_groups=mesh['dp'=4,'ctx'=2,'tp'=4] {'dp','ctx'}, use_global_device_ids=true, to_apply=%region_21.22.clone | all-reduce | flops 4096 | bytes 32768
  506.6 7.3 fusion.82
  513.9 17.9 %reduce-scatter.13.cloned.1.call-done = f32[256,64]{0,1:T(8,128)} async-done(((f32[2048,64]{0,1:T(8,128)}), f32[256,64]{0,1:T(8,128)}) %reduce-scatter.13.cloned.1.call-update) | async-done | bytes 65552 | tf_op jit(solution)/shard_map/reduce_scatter | solution.py:255
  531.8 66.0 %reduce-scatter.15.cloned.1.call-done = f32[256,64]{0,1:T(8,128)} async-done(((f32[2048,64]{0,1:T(8,128)}), f32[256,64]{0,1:T(8,128)}) %reduce-scatter.15.cloned.1.call-update) | async-done | bytes 65552 | tf_op jit(solution)/shard_map/reduce_scatter | solution.py:256
  597.8 91.6 %reduce-scatter.11.cloned.1.call-done = f32[256,512]{1,0:T(8,128)} async-done(((f32[2048,512]{1,0:T(8,128)}), f32[256,512]{1,0:T(8,128)}) %reduce-scatter.11.cloned.1.call-update) | async-done | bytes 524304 | tf_op jit(solution)/shard_map/reduce_scatter | solution.py:254
  689.4 92.6 %reduce-scatter.17.cloned.1.call-done = f32[512,256]{1,0:T(8,128)} async-done(((f32[512,2048]{1,0:T(8,128)}), f32[512,256]{1,0:T(8,128)}) %reduce-scatter.17.cloned.1.call-update) | async-done | bytes 524304 | tf_op jit(solution)/shard_map/reduce_scatter | solution.py:257
  781.9 196.4 %reduce-scatter.21.cloned.1.call-done = f32[256,1408]{1,0:T(8,128)} async-done(((f32[2048,1408]{1,0:T(8,128)}), f32[256,1408]{1,0:T(8,128)}) %reduce-scatter.21.cloned.1.call-update) | async-done | bytes 1441808 | tf_op jit(solution)/shard_map/reduce_scatter | solution.py:260
  978.4 196.1 %reduce-scatter.19.cloned.1.call-done = f32[256,1408]{1,0:T(8,128)} async-done(((f32[2048,1408]{1,0:T(8,128)}), f32[256,1408]{1,0:T(8,128)}) %reduce-scatter.19.cloned.1.call-update) | async-done | bytes 1441808 | tf_op jit(solution)/shard_map/reduce_scatter | solution.py:259
  1174.4 196.4 %reduce-scatter.23.cloned.1.call-done = f32[1408,256]{1,0:T(8,128)} async-done(((f32[1408,2048]{1,0:T(8,128)}), f32[1408,256]{1,0:T(8,128)}) %reduce-scatter.23.cloned.1.call-update) | async-done | bytes 1441808 | tf_op jit(solution)/shard_map/reduce_scatter | solution.py:261
  (245 shorter events, 102.5 us)
Async XLA Ops:
  7.2 46.3 %copy-start = (bf16[512,2048]{1,0:T(8,128)(2,1)S(1)}, bf16[512,2048]{1,0:T(8,128)(2,1)}, u32[]{:S(2)}) copy-start(bf16[512,2048]{1,0:T(8,128)(2,1)} %param.26) | copy-start | bytes 6291460
  7.2 136.7 %all-reduce.8.cloned.1.call-start = ((), (), s32[]{:S(2)}) async-start(), calls=%async_computation.8 | async-start | bytes 8388608 | tf_op jit(solution)/shard_map/psum | solution.py:143
  12.3 11.2 copy-start.2
  14.9 11.1 copy-start.19
  56.8 90.7 %copy-start.38 = (f32[2048]{0:T(1024)S(1)}, f32[2048]{0:T(1024)}, u32[]{:S(2)}) copy-start(f32[2048]{0:T(1024)} %param.27) | copy-start | bytes 24580
  56.8 210.0 %all-reduce.12.cloned.1.call-start = ((), (), s32[]{:S(2)}) async-start(), calls=%async_computation.10 | async-start | bytes 8388608 | tf_op jit(solution)/shard_map/psum | solution.py:163
  147.4 10.5 copy-start.4
  147.4 10.5 slice-start
  147.4 15.6 %slice-start.4 = ((s8[5767168]{0:T(1024)(128)(4,1)}), s8[4194304]{0:T(1024)(128)(4,1)S(1)}, s32[]{:S(2)}) async-start(s8[5767168]{0:T(1024)(128)(4,1)} %bitcast.337), calls=%async_computation.24 | async-start | bytes 8388608
  147.9 15.1 %slice-start.5 = ((s8[5767168]{0:T(1024)(128)(4,1)}), s8[1572864]{0:T(1024)(128)(4,1)S(1)}, s32[]{:S(2)}) async-start(s8[5767168]{0:T(1024)(128)(4,1)} %bitcast.337), calls=%async_computation.25 | async-start | bytes 3145728
  158.0 18.0 %slice-start.2 = ((s8[5767168]{0:T(1024)(128)(4,1)}), s8[4194304]{0:T(1024)(128)(4,1)S(1)}, s32[]{:S(2)}) async-start(s8[5767168]{0:T(1024)(128)(4,1)} %bitcast.335), calls=%async_computation.22 | async-start | bytes 8388608
  163.0 13.0 slice-start.3
  181.0 139.7 %all-reduce.10.cloned.1.call-start = ((), (), s32[]{:S(2)}) async-start(), calls=%async_computation.9 | async-start | bytes 4194304 | tf_op jit(solution)/shard_map/psum | solution.py:151
  188.9 184.4 %reduce-scatter.9.cloned.1.call-start = ((), (), s32[]{:S(2)}) async-start(), calls=%async_computation.11 | async-start | bytes 786432 | tf_op jit(solution)/shard_map/reduce_scatter | solution.py:229
  339.6 19.2 %copy-start.20 = (f32[512,64]{0,1:T(8,128)S(1)}, f32[512,64]{0,1:T(8,128)}, u32[]{:S(2)}) copy-start(f32[512,64]{0,1:T(8,128)} %copy-done.19) | copy-start | bytes 393220
  358.5 106.3 %all-reduce.14.cloned.1.call-start = ((), (), s32[]{:S(2)}) async-start(), calls=%async_computation.12 | async-start | bytes 8388608 | tf_op jit(solution)/shard_map/psum | solution.py:244
  360.3 13.0 copy-start.31
  360.3 14.1 %copy-start.33 = (f32[512,32]{0,1:T(8,128)S(1)}, f32[512,32]{0,1:T(8,128)}, u32[]{:S(2)}) copy-start(f32[512,32]{0,1:T(8,128)} %copy-done.32) | copy-start | bytes 196612
  360.3 15.4 %copy-start.24 = (bf16[2048,64]{0,1:T(8,128)(2,1)S(1)}, bf16[2048,64]{0,1:T(8,128)(2,1)}, u32[]{:S(2)}) copy-start(bf16[2048,64]{0,1:T(8,128)(2,1)} %param.24) | copy-start | bytes 786436
  363.6 12.8 copy-start.26
  379.1 152.6 %reduce-scatter.13.cloned.1.call-start = ((), (), s32[]{:S(2)}) async-start(), calls=%async_computation.14 | async-start | bytes 589824 | tf_op jit(solution)/shard_map/reduce_scatter | solution.py:255
  382.0 215.8 %reduce-scatter.15.cloned.1.call-start = ((), (), s32[]{:S(2)}) async-start(), calls=%async_computation.15 | async-start | bytes 589824 | tf_op jit(solution)/shard_map/reduce_scatter | solution.py:256
  383.4 306.0 %reduce-scatter.11.cloned.1.call-start = ((), (), s32[]{:S(2)}) async-start(), calls=%async_computation.13 | async-start | bytes 4718592 | tf_op jit(solution)/shard_map/reduce_scatter | solution.py:254
  386.7 395.2 %reduce-scatter.17.cloned.1.call-start = ((), (), s32[]{:S(2)}) async-start(), calls=%async_computation.16 | async-start | bytes 4718592 | tf_op jit(solution)/shard_map/reduce_scatter | solution.py:257
  393.3 585.0 %reduce-scatter.21.cloned.1.call-start = ((), (), s32[]{:S(2)}) async-start(), calls=%async_computation.18 | async-start | bytes 12976128 | tf_op jit(solution)/shard_map/reduce_scatter | solution.py:260
  401.6 772.8 %reduce-scatter.19.cloned.1.call-start = ((), (), s32[]{:S(2)}) async-start(), calls=%async_computation.17 | async-start | bytes 12976128 | tf_op jit(solution)/shard_map/reduce_scatter | solution.py:259
  409.3 961.5 %reduce-scatter.23.cloned.1.call-start = ((), (), s32[]{:S(2)}) async-start(), calls=%async_computation.19 | async-start | bytes 12976128 | tf_op jit(solution)/shard_map/reduce_scatter | solution.py:261
  417.3 47.5 %copy-start.5 = (bf16[512,2048]{1,0:T(8,128)(2,1)S(1)}, bf16[512,2048]{1,0:T(8,128)(2,1)}, u32[]{:S(2)}) copy-start(bf16[512,2048]{1,0:T(8,128)(2,1)} %param.20) | copy-start | bytes 6291460
  417.3 47.5 %copy-start.37 = (f32[2048]{0:T(1024)S(1)}, f32[2048]{0:T(1024)}, u32[]{:S(2)}) copy-start(f32[2048]{0:T(1024)} %param.22) | copy-start | bytes 24580
  417.3 47.5 %copy-start.41 = (f32[512]{0:T(512)S(1)}, f32[512]{0:T(512)}, u32[]{:S(2)}) copy-start(f32[512]{0:T(512)} %copy-done.40) | copy-start | bytes 6148
  417.4 50.7 %copy-start.39 = (f32[2048]{0:T(1024)S(1)}, f32[2048]{0:T(1024)}, u32[]{:S(2)}) copy-start(f32[2048]{0:T(1024)} %get-tuple-element.835) | copy-start | bytes 24580
  506.6 864.2 %copy-start.1 = (bf16[512,2048]{1,0:T(8,128)(2,1)S(1)}, bf16[512,2048]{1,0:T(8,128)(2,1)}, u32[]{:S(2)}) copy-start(bf16[512,2048]{1,0:T(8,128)(2,1)} %param.26) | copy-start | bytes 6291460
  (39 other events, 109.5 us)
Sparse Core Ops, SparseCore 0:
  56.9 86.9 all-reduce.7
  181.2 85.5 all-reduce.11
  269.2 51.5 all-reduce.9
  358.6 14.6 reduce-scatter.8
  379.3 85.4 all-reduce.13
  468.6 63.1 reduce-scatter.12
  535.7 62.0 reduce-scatter.14
  602.0 87.3 reduce-scatter.10
  693.6 88.3 reduce-scatter.16
  785.9 192.3 reduce-scatter.20
  982.5 191.8 reduce-scatter.18
  1178.4 192.3 reduce-scatter.22
where the time goes:
time: 1380 us
  waiting for transfers between devices  1130 us (82%)
  matrix products  122 us (9%)
  other arithmetic  48.4 us (4%)
  blocking collectives  44.5 us (3%)
  local copies, waits for them, and re-layouts  19.5 us (1%)
  between operations  15.7 us (1%)
    reduce_scatter x1, waiting for transfers between devices, shards(): lax.psum_scatter(mlp_done[1], ('dp', 'ctx'), scatter_dimension=0, tiled=T...  196 us
    reduce_scatter x1, waiting for transfers between devices, shards(): lax.psum_scatter(mlp_done[2], ('dp', 'ctx'), scatter_dimension=1, tiled=T...  196 us
    reduce_scatter x1, waiting for transfers between devices, shards(): lax.psum_scatter(mlp_done[0], ('dp', 'ctx'), scatter_dimension=0, tiled=T...  196 us
    reduce_scatter x1, waiting for transfers between devices, shards(): lax.psum_scatter(output_grad, ('dp', 'ctx'), scatter_dimension=1, tiled=T...  92.6 us
    reduce_scatter x1, waiting for transfers between devices, shards(): lax.psum_scatter(query_grad, ('dp', 'ctx'), scatter_dimension=0, tiled=True)  91.6 us
    psum x1, waiting for transfers between devices, shards(): branch = lax.psum(contract(heads_out, output_weight, 1, 0), 'tp')  86.9 us
    dot_general x21, matrix products, contract(): lax.dot_general(left_side, right_side, (((left_dim,), (right_dim,)), ((),...  84.8 us
    psum x1, waiting for transfers between devices, shards(): lax.psum(contract(gate_back, gate_weight, 1, 1) + contract(up_back, up_we...  77.4 us
  transfers between devices with their start and end apart: 12, of which 12 were waited for; matrix products, arithmetic and copies ran while one was open for 4% of the time, Pallas kernels for 0%

commit v1 on v0

--- a/solution.py
+++ b/solution.py
@@ -140,7 +140,7 @@
         0, ctx_count, out_step, jnp.zeros((row_count, kv_local, groups, HEAD), jnp.float32)
     )
     heads_out = mixed_heads.reshape(row_count, q_local * HEAD).astype(jnp.bfloat16)
-    branch = lax.psum(contract(heads_out, output_weight, 1, 0), "tp")
+    branch = jnp.sum(lax.all_gather(contract(heads_out, output_weight, 1, 0), "tp"), axis=0)
     middle = tokens_wide + branch
     normed_two, inverse_two, mlp_in = rms_parts(middle, mlp_gain)
     gate_pre = contract(mlp_in, gate_weight, 1, 0)

time: 1380 us -> 1410 us (1.022)
    all_gather x0 -> x1, waiting for transfers between devices: none -> 107 us  [shards(): lax.all_gather(contract(heads_out, output_weight, 1, 0), 'tp')]
    psum x1 -> x0, waiting for transfers between devices: 86.9 us -> none  [shards(): branch = lax.psum(contract(heads_out, output_weight, 1, 0), 'tp')]
where the time goes in v1:
time: 1410 us
  waiting for transfers between devices  1140 us (81%)
  matrix products  126 us (9%)
  other arithmetic  58.5 us (4%)
  blocking collectives  44.5 us (3%)
  local copies, waits for them, and re-layouts  17.9 us (1%)
  between operations  15.7 us (1%)
    reduce_scatter x1, waiting for transfers between devices, shards(): lax.psum_scatter(mlp_done[1], ('dp', 'ctx'), scatter_dimension=0, tiled=T...  196 us
    reduce_scatter x1, waiting for transfers between devices, shards(): lax.psum_scatter(mlp_done[2], ('dp', 'ctx'), scatter_dimension=1, tiled=T...  196 us
    reduce_scatter x1, waiting for transfers between devices, shards(): lax.psum_scatter(mlp_done[0], ('dp', 'ctx'), scatter_dimension=0, tiled=T...  196 us
    all_gather x1, waiting for transfers between devices, shards(): lax.all_gather(contract(heads_out, output_weight, 1, 0), 'tp')  107 us
    reduce_scatter x1, waiting for transfers between devices, shards(): lax.psum_scatter(output_grad, ('dp', 'ctx'), scatter_dimension=1, tiled=T...  92.6 us
    reduce_scatter x1, waiting for transfers between devices, shards(): lax.psum_scatter(query_grad, ('dp', 'ctx'), scatter_dimension=0, tiled=True)  91.6 us
    dot_general x21, matrix products, contract(): lax.dot_general(left_side, right_side, (((left_dim,), (right_dim,)), ((),...  89.1 us
    psum x1, waiting for transfers between devices, shards(): lax.psum(contract(gate_back, gate_weight, 1, 1) + contract(up_back, up_we...  77.7 us
  transfers between devices with their start and end apart: 12, of which 12 were waited for; matrix products, arithmetic and copies ran while one was open for 4% of the time, Pallas kernels for 0%

profile of v1, /device:TPU:0, one launch (start us, length us, event | category | flops | bytes accessed | tf_op | source)
XLA Modules:
  0.0 1409.2 jit_solution(8397396174476878567)
XLA Ops:
  14.3 7.3 all_gather.9
  27.1 11.2 while.60
  39.0 12.4 while.61
  46.3 5.1 fusion.177
  57.1 107.3 %all-gather.3.cloned.1.call-done = f32[2048,2048]{1,0:T(8,128)} async-done(((f32[512,2048]{1,0:T(8,128)}), f32[2048,2048]{1,0:T(8,128)}) %all-gather.3.cloned.1.call-update) | async-done | bytes 16777232 | tf_op jit(solution)/shard_map/all_gather | solution.py:143
  164.4 10.2 reduce_sum.90
  178.6 10.0 fusion.104
  188.7 5.0 fusion.103
  193.7 8.3 multiply_convert_fusion.1
  206.9 5.0 convolution_add_fusion
  212.0 7.8 convolution_convert_fusion
  219.9 77.7 %all-reduce.9.cloned.1.call-done = f32[512,2048]{1,0:T(8,128)} async-done(((f32[512,2048]{1,0:T(8,128)}), f32[512,2048]{1,0:T(8,128)}) %all-reduce.9.cloned.1.call-update) | async-done | bytes 4194320 | tf_op jit(solution)/shard_map/psum | solution.py:163
  297.6 5.0 multiply_reduce_fusion
  302.7 48.9 %all-reduce.7.cloned.1.call-done = bf16[512,2048]{1,0:T(8,128)(2,1)} async-done(((bf16[512,2048]{1,0:T(8,128)(2,1)}), bf16[512,2048]{1,0:T(8,128)(2,1)}) %all-reduce.7.cloned.1.call-update) | async-done | bytes 2097168 | tf_op jit(solution)/shard_map/psum | solution.py:151
  351.6 7.4 multiply_add_fusion
  361.0 9.2 while.62
  370.8 18.1 %while.63 = (s32[]{:T(128)}, f32[512,1,8,64]{0,3,2,1:T(8,128)S(1)}, f32[1024,128]{0,1:T(8,128)S(1)}, bf16[1024,128]{0,1:T(8,128)(2,1)S(1)}, s32[512]{0:T(512)S(1...) while((s32[]{:T(128)}, f32[512,1,8,64]{0,3,2,1:T(8,128)S(1)}, ...), condition=%wide.region_16.17_spmd.clone, body=%wide.region_15.16_spmd.clone.sunk | while | flops 1364886528 | bytes 44171576 | solution.py:228
  394.9 9.8 reduce-scatter.9.cloned.1.call-done
  419.0 5.5 fusion.89
  426.2 7.6 fusion.110
  433.9 7.6 fusion.109
  443.1 7.4 fusion.111
  452.3 43.8 %all-reduce.11.cloned.1.call-done = f32[512,2048]{1,0:T(8,128)} async-done(((f32[512,2048]{1,0:T(8,128)}), f32[512,2048]{1,0:T(8,128)}) %all-reduce.11.cloned.1.call-update) | async-done | bytes 4194320 | tf_op jit(solution)/shard_map/psum | solution.py:244
  499.4 37.2 %all-reduce.2 = (f32[2048]{0:T(1024)S(1)}, f32[2048]{0:T(1024)S(1)}) all-reduce(f32[2048]{0:T(1024)S(1)} %get-tuple-element.837, f32[2048]{0:T(1024)S(1)} %copy-done.40), channel_id=4, replica_groups=mesh['dp'=4,'ctx'=2,'tp'=4] {'dp','ctx'}, use_global_device_ids=true, to_apply=%region_21.22.clone | all-reduce | flops 4096 | bytes 32768
  537.9 7.3 fusion.82
  545.2 17.9 %reduce-scatter.13.cloned.1.call-done = f32[256,64]{0,1:T(8,128)} async-done(((f32[2048,64]{0,1:T(8,128)}), f32[256,64]{0,1:T(8,128)}) %reduce-scatter.13.cloned.1.call-update) | async-done | bytes 65552 | tf_op jit(solution)/shard_map/reduce_scatter | solution.py:255
  563.1 66.0 %reduce-scatter.15.cloned.1.call-done = f32[256,64]{0,1:T(8,128)} async-done(((f32[2048,64]{0,1:T(8,128)}), f32[256,64]{0,1:T(8,128)}) %reduce-scatter.15.cloned.1.call-update) | async-done | bytes 65552 | tf_op jit(solution)/shard_map/reduce_scatter | solution.py:256
  629.0 91.6 %reduce-scatter.11.cloned.1.call-done = f32[256,512]{1,0:T(8,128)} async-done(((f32[2048,512]{1,0:T(8,128)}), f32[256,512]{1,0:T(8,128)}) %reduce-scatter.11.cloned.1.call-update) | async-done | bytes 524304 | tf_op jit(solution)/shard_map/reduce_scatter | solution.py:254
  720.7 92.6 %reduce-scatter.17.cloned.1.call-done = f32[512,256]{1,0:T(8,128)} async-done(((f32[512,2048]{1,0:T(8,128)}), f32[512,256]{1,0:T(8,128)}) %reduce-scatter.17.cloned.1.call-update) | async-done | bytes 524304 | tf_op jit(solution)/shard_map/reduce_scatter | solution.py:257
  813.2 196.4 %reduce-scatter.21.cloned.1.call-done = f32[256,1408]{1,0:T(8,128)} async-done(((f32[2048,1408]{1,0:T(8,128)}), f32[256,1408]{1,0:T(8,128)}) %reduce-scatter.21.cloned.1.call-update) | async-done | bytes 1441808 | tf_op jit(solution)/shard_map/reduce_scatter | solution.py:260
  1009.7 196.1 %reduce-scatter.19.cloned.1.call-done = f32[256,1408]{1,0:T(8,128)} async-done(((f32[2048,1408]{1,0:T(8,128)}), f32[256,1408]{1,0:T(8,128)}) %reduce-scatter.19.cloned.1.call-update) | async-done | bytes 1441808 | tf_op jit(solution)/shard_map/reduce_scatter | solution.py:259
  1205.7 196.4 %reduce-scatter.23.cloned.1.call-done = f32[1408,256]{1,0:T(8,128)} async-done(((f32[1408,2048]{1,0:T(8,128)}), f32[1408,256]{1,0:T(8,128)}) %reduce-scatter.23.cloned.1.call-update) | async-done | bytes 1441808 | tf_op jit(solution)/shard_map/reduce_scatter | solution.py:261
  (242 shorter events, 105.0 us)
Async XLA Ops:
  7.2 46.3 %copy-start = (bf16[512,2048]{1,0:T(8,128)(2,1)S(1)}, bf16[512,2048]{1,0:T(8,128)(2,1)}, u32[]{:S(2)}) copy-start(bf16[512,2048]{1,0:T(8,128)(2,1)} %param.26) | copy-start | bytes 6291460
  7.2 157.2 %all-gather.3.cloned.1.call-start = ((), (), s32[]{:S(2)}) async-start(), calls=%async_computation.19 | async-start | bytes 20971520 | tf_op jit(solution)/shard_map/all_gather | solution.py:143
  11.7 11.2 copy-start.2
  14.3 11.1 copy-start.19
  56.8 240.8 %all-reduce.9.cloned.1.call-start = ((), (), s32[]{:S(2)}) async-start(), calls=%async_computation.9 | async-start | bytes 8388608 | tf_op jit(solution)/shard_map/psum | solution.py:163
  178.1 10.6 copy-start.4
  178.1 10.5 slice-start
  178.1 15.6 %slice-start.4 = ((s8[5767168]{0:T(1024)(128)(4,1)}), s8[4194304]{0:T(1024)(128)(4,1)S(1)}, s32[]{:S(2)}) async-start(s8[5767168]{0:T(1024)(128)(4,1)} %bitcast.339), calls=%async_computation.24 | async-start | bytes 8388608
  178.5 10.1 copy-start.13
  178.6 15.1 %slice-start.5 = ((s8[5767168]{0:T(1024)(128)(4,1)}), s8[1572864]{0:T(1024)(128)(4,1)S(1)}, s32[]{:S(2)}) async-start(s8[5767168]{0:T(1024)(128)(4,1)} %bitcast.339), calls=%async_computation.25 | async-start | bytes 3145728
  188.6 18.3 %slice-start.2 = ((s8[5767168]{0:T(1024)(128)(4,1)}), s8[4194304]{0:T(1024)(128)(4,1)S(1)}, s32[]{:S(2)}) async-start(s8[5767168]{0:T(1024)(128)(4,1)} %bitcast.337), calls=%async_computation.22 | async-start | bytes 8388608
  193.7 13.2 slice-start.3
  212.0 139.6 %all-reduce.7.cloned.1.call-start = ((), (), s32[]{:S(2)}) async-start(), calls=%async_computation.8 | async-start | bytes 4194304 | tf_op jit(solution)/shard_map/psum | solution.py:151
  219.9 184.7 %reduce-scatter.9.cloned.1.call-start = ((), (), s32[]{:S(2)}) async-start(), calls=%async_computation.10 | async-start | bytes 786432 | tf_op jit(solution)/shard_map/reduce_scatter | solution.py:229
  370.8 19.2 %copy-start.20 = (f32[512,64]{0,1:T(8,128)S(1)}, f32[512,64]{0,1:T(8,128)}, u32[]{:S(2)}) copy-start(f32[512,64]{0,1:T(8,128)} %copy-done.19) | copy-start | bytes 393220
  389.8 106.3 %all-reduce.11.cloned.1.call-start = ((), (), s32[]{:S(2)}) async-start(), calls=%async_computation.11 | async-start | bytes 8388608 | tf_op jit(solution)/shard_map/psum | solution.py:244
  391.6 13.0 copy-start.31
  391.6 14.1 %copy-start.33 = (f32[512,32]{0,1:T(8,128)S(1)}, f32[512,32]{0,1:T(8,128)}, u32[]{:S(2)}) copy-start(f32[512,32]{0,1:T(8,128)} %copy-done.32) | copy-start | bytes 196612
  391.6 15.4 %copy-start.24 = (bf16[2048,64]{0,1:T(8,128)(2,1)S(1)}, bf16[2048,64]{0,1:T(8,128)(2,1)}, u32[]{:S(2)}) copy-start(bf16[2048,64]{0,1:T(8,128)(2,1)} %param.24) | copy-start | bytes 786436
  394.9 12.8 copy-start.26
  410.4 152.6 %reduce-scatter.13.cloned.1.call-start = ((), (), s32[]{:S(2)}) async-start(), calls=%async_computation.13 | async-start | bytes 589824 | tf_op jit(solution)/shard_map/reduce_scatter | solution.py:255
  413.3 215.8 %reduce-scatter.15.cloned.1.call-start = ((), (), s32[]{:S(2)}) async-start(), calls=%async_computation.14 | async-start | bytes 589824 | tf_op jit(solution)/shard_map/reduce_scatter | solution.py:256
  414.6 306.0 %reduce-scatter.11.cloned.1.call-start = ((), (), s32[]{:S(2)}) async-start(), calls=%async_computation.12 | async-start | bytes 4718592 | tf_op jit(solution)/shard_map/reduce_scatter | solution.py:254
  418.0 395.2 %reduce-scatter.17.cloned.1.call-start = ((), (), s32[]{:S(2)}) async-start(), calls=%async_computation.15 | async-start | bytes 4718592 | tf_op jit(solution)/shard_map/reduce_scatter | solution.py:257
  424.6 585.0 %reduce-scatter.21.cloned.1.call-start = ((), (), s32[]{:S(2)}) async-start(), calls=%async_computation.17 | async-start | bytes 12976128 | tf_op jit(solution)/shard_map/reduce_scatter | solution.py:260
  433.8 771.9 %reduce-scatter.19.cloned.1.call-start = ((), (), s32[]{:S(2)}) async-start(), calls=%async_computation.16 | async-start | bytes 12976128 | tf_op jit(solution)/shard_map/reduce_scatter | solution.py:259
  441.5 960.6 %reduce-scatter.23.cloned.1.call-start = ((), (), s32[]{:S(2)}) async-start(), calls=%async_computation.18 | async-start | bytes 12976128 | tf_op jit(solution)/shard_map/reduce_scatter | solution.py:261
  450.4 45.7 %copy-start.5 = (bf16[512,2048]{1,0:T(8,128)(2,1)S(1)}, bf16[512,2048]{1,0:T(8,128)(2,1)}, u32[]{:S(2)}) copy-start(bf16[512,2048]{1,0:T(8,128)(2,1)} %param.20) | copy-start | bytes 6291460
  450.4 45.7 %copy-start.38 = (f32[2048]{0:T(1024)S(1)}, f32[2048]{0:T(1024)}, u32[]{:S(2)}) copy-start(f32[2048]{0:T(1024)} %param.22) | copy-start | bytes 24580
  450.4 45.7 %copy-start.42 = (f32[512]{0:T(512)S(1)}, f32[512]{0:T(512)}, u32[]{:S(2)}) copy-start(f32[512]{0:T(512)} %copy-done.41) | copy-start | bytes 6148
  450.5 48.9 %copy-start.40 = (f32[2048]{0:T(1024)S(1)}, f32[2048]{0:T(1024)}, u32[]{:S(2)}) copy-start(f32[2048]{0:T(1024)} %get-tuple-element.835) | copy-start | bytes 24580
  537.9 864.2 %copy-start.1 = (bf16[512,2048]{1,0:T(8,128)(2,1)S(1)}, bf16[512,2048]{1,0:T(8,128)(2,1)}, u32[]{:S(2)}) copy-start(bf16[512,2048]{1,0:T(8,128)(2,1)} %param.26) | copy-start | bytes 6291460
  (37 other events, 114.3 us)
Sparse Core Ops, SparseCore 0:
  56.9 107.3 all-gather.2
  212.1 85.4 all-reduce.8
  300.0 51.5 all-reduce.6
  389.9 14.6 reduce-scatter.8
  410.5 85.4 all-reduce.10
  499.8 63.1 reduce-scatter.12
  567.0 62.0 reduce-scatter.14
  633.2 87.3 reduce-scatter.10
  724.9 88.3 reduce-scatter.16
  817.2 192.3 reduce-scatter.20
  1013.8 191.8 reduce-scatter.18
  1209.7 192.3 reduce-scatter.22
